TPU v7x, 32 devices: a whole 2x2x4 slice. The times are simulated.
32 devices in a mesh: gx: 4 (over y, x), gy: 8 (over z, core).
Axes of the slice: x: 2, y: 2, z: 4, core: 2. Of those that a mesh axis runs over, the one named last changes fastest.
Arguments:
- e_field: float32 [3, 128, 256, 128], P(None, 'gx', 'gy'), may hold values from -6 to 6
- h_field: float32 [3, 128, 256, 128], P(None, 'gx', 'gy'), may hold values from -6 to 6
- psi: float32 [12, 128, 256, 128], P(None, 'gx', 'gy'), may hold values from -6 to 6
- material: int32 [128, 256, 128], P('gx', 'gy'), may hold values from 0 to 7
- eps_table: float32 [8], replicated, may hold values from 1 to 1.2
- sigma_table: float32 [8], replicated, may hold values from 0 to 0.05
Outputs:
- e_out: float32 [3, 128, 256, 128], P(None, 'gx', 'gy')
- h_out: float32 [3, 128, 256, 128], P(None, 'gx', 'gy')
- psi_out: float32 [12, 128, 256, 128], P(None, 'gx', 'gy')
All inputs are finite; a program needn't handle non-finite values.
Results may differ from a plain program's by a relative error of at most 0.0003.
Values sent between devices are 32-bit elements; how exact they have to be, the bound alone decides.
A program may use at most 128 MiB of HBM per device.

v0:
```python
import jax
import jax.numpy as jnp
from jax import lax
from jax.sharding import PartitionSpec as P

PML = 16
STEPS = 16
NMAT = 8


time_step = 0.5
sigma_peak = 3.0
kappa_peak = 5.0
alpha_peak = 0.05
curl_table = (((2, 1), (1, 2)), ((0, 2), (2, 0)), ((1, 0), (0, 1)))


def shifted_2(shard, axis, by):
    size = lax.axis_size(axis)
    pairs = [(i, i + by) for i in range(size) if 0 <= i + by < size]
    return lax.ppermute(shard, axis, pairs)


def profile(length, offset, extent, shift_half, thickness):
    position = (offset + lax.iota(jnp.int32, length)).astype(jnp.float32) + shift_half
    slab_width = jnp.float32(thickness)
    depth_frac = jnp.maximum(
        jnp.maximum(
            (slab_width - position) / slab_width, (position - (extent - slab_width)) / slab_width
        ),
        0.0,
    )
    depth_cube = depth_frac * depth_frac * depth_frac
    sigma_value = sigma_peak * depth_cube
    kappa_value = 1.0 + (kappa_peak - 1.0) * depth_cube
    alpha_value = alpha_peak * (1.0 - depth_frac)
    decays = jnp.exp(-(sigma_value / kappa_value + alpha_value) * time_step)
    scaling = (
        sigma_value * (decays - 1.0) / (kappa_value * (sigma_value + kappa_value * alpha_value))
    )
    inside_slab = depth_frac > 0.0
    return (
        jnp.where(inside_slab, decays, 0.0),
        jnp.where(inside_slab, scaling, 0.0),
        1.0 / kappa_value,
    )


def shaped(vector, direction):
    target_shape = [1, 1, 1]
    target_shape[direction] = vector.shape[0]
    return vector.reshape(target_shape)


def forward(field, direction, following):
    shifted = lax.slice_in_dim(field, 1, field.shape[direction], axis=direction)
    return jnp.concatenate([shifted, following], axis=direction) - field


def backward(field, direction, preceding):
    shifted = lax.slice_in_dim(field, 0, field.shape[direction] - 1, axis=direction)
    return field - jnp.concatenate([preceding, shifted], axis=direction)


def zero_layer(field, direction):
    return jnp.zeros_like(lax.slice_in_dim(field, 0, 1, axis=direction))


def plain_term(difference, auxiliary, coefficient, direction):
    decays, scaling, inverse = coefficient
    renewed = decays * auxiliary + scaling * difference
    return (inverse * difference + renewed, renewed)


def curl(difference_of, auxiliary, first_slot, coefficients, renew):
    results = []
    renewed_list = []
    for component in range(3):
        plus_pair, minus_pair = curl_table[component]
        slot = first_slot + 2 * component
        plus_value, plus_aux = renew(
            difference_of(plus_pair[0], plus_pair[1]),
            auxiliary[slot],
            coefficients[plus_pair[1]],
            plus_pair[1],
        )
        minus_value, minus_aux = renew(
            difference_of(minus_pair[0], minus_pair[1]),
            auxiliary[slot + 1],
            coefficients[minus_pair[1]],
            minus_pair[1],
        )
        results.append(plus_value - minus_value)
        renewed_list.append(plus_aux)
        renewed_list.append(minus_aux)
    return (results, renewed_list)


def material_coefficients(material, eps_table, sigma_table):
    losses = sigma_table * time_step / (2.0 * eps_table)
    keep_table = (1.0 - losses) / (1.0 + losses)
    drive_table = time_step / eps_table / (1.0 + losses)
    keeping = jnp.zeros(material.shape, jnp.float32)
    driving = jnp.zeros(material.shape, jnp.float32)
    for number in range(NMAT):
        chosen = material == number
        keeping = keeping + jnp.where(chosen, keep_table[number], 0.0)
        driving = driving + jnp.where(chosen, drive_table[number], 0.0)
    return (keeping, driving)


def profiles_for(layout):
    magnetic_coef = [
        tuple(
            (
                shaped(vector, direction)
                for vector in profile(
                    layout[direction][0], layout[direction][1], layout[direction][2], 0.5, PML
                )
            )
        )
        for direction in range(3)
    ]
    electric_coef = [
        tuple(
            (
                shaped(vector, direction)
                for vector in profile(
                    layout[direction][0], layout[direction][1], layout[direction][2], 0.0, PML
                )
            )
        )
        for direction in range(3)
    ]
    return (magnetic_coef, electric_coef)


def shards(e_field, h_field, psi, material, eps_table, sigma_table):
    rows_x = e_field.shape[1]
    rows_y = e_field.shape[2]
    depth_z = e_field.shape[3]
    extent_x = lax.axis_size("gx") * rows_x
    extent_y = lax.axis_size("gy") * rows_y
    layout = (
        (rows_x, lax.axis_index("gx") * rows_x, extent_x),
        (rows_y, lax.axis_index("gy") * rows_y, extent_y),
        (depth_z, 0, depth_z),
    )
    magnetic_coef, electric_coef = profiles_for(layout)
    keeping, driving = material_coefficients(material, eps_table, sigma_table)

    def advance(turn_index, carry):
        electric, magnetic, auxiliary = carry
        front_x = electric[1:3, :1]
        front_y = electric[0::2, :, :1]
        after_x = shifted_2(front_x, "gx", -1)
        after_y = shifted_2(front_y, "gy", -1)

        def electric_ahead(source, direction):
            field = electric[source]
            if direction == 0:
                return forward(field, 0, after_x[source - 3])
            if direction == 1:
                return forward(field, 1, after_y[0 if source == 0 else -1])
            return forward(field, 2, zero_layer(field, 2))

        curl_h, renewed_h = curl(electric_ahead, auxiliary, 0, magnetic_coef, plain_term)
        magnetic_new = jnp.stack(
            [magnetic[component] - time_step * curl_h[component] for component in range(3)]
        )
        rear_x = magnetic_new[1:3, -1:]
        rear_y = magnetic_new[0::2, :, -1:]
        before_x = shifted_2(rear_x, "gx", 1)
        before_y = shifted_2(rear_y, "gy", 1)

        def magnetic_behind(source, direction):
            field = magnetic_new[source]
            if direction == 0:
                return backward(field, 0, before_x[source - 3])
            if direction == 1:
                return backward(field, 1, before_y[0 if source == 0 else -1])
            return backward(field, 2, zero_layer(field, 2))

        curl_e, renewed_e = curl(magnetic_behind, auxiliary, 6, electric_coef, plain_term)
        electric_new = jnp.stack(
            [keeping * electric[component] + driving * curl_e[component] for component in range(3)]
        )
        return (electric_new, magnetic_new, jnp.stack(renewed_h + renewed_e))

    e_out, h_out, psi_out = lax.fori_loop(0, STEPS, advance, (e_field, h_field, psi))
    return (e_out, h_out, psi_out)


def solution(mesh):
    in_specs = (
        P(None, "gx", "gy", None),
        P(None, "gx", "gy", None),
        P(None, "gx", "gy", None),
        P("gx", "gy", None),
        P(),
        P(),
    )
    out_specs = (P(None, "gx", "gy", None), P(None, "gx", "gy", None), P(None, "gx", "gy", None))
    return jax.shard_map(shards, mesh=mesh, in_specs=in_specs, out_specs=out_specs, check_vma=False)
```

profile of v0, /device:TPU:5, one launch (start us, length us, event | category | flops | bytes accessed | tf_op | source)
XLA Modules:
  0.0 508.2 jit_solution(321116058230156544)
XLA Ops:
  0.7 6.3 %copy.42 = f32[12,32,32,128]{3,2,1,0:T(8,128)} copy(f32[12,32,32,128]{3,2,1,0:T(8,128)} %param.10) | data formatting | bytes 12582912
  8.8 5.8 %select_add_fusion = (f32[32,32,128]{2,1,0:T(8,128)S(1)}, pred[32,32,128]{2,1,0:T(8,128)(4,1)S(1)}, pred[32,32,128]{2,1,0:T(8,128)(4,1)S(1)}, pred[32,32,128]{2,...) fusion(f32[]{:T(128)} %bitcast.15, f32[]{:T(128)} %bitcast.14, ...), kind=kLoop, calls=%fused_computation.189 | loop fusion | flops 3014656 | bytes 2097184 | tf_op jit(solution)/shard_map/add | solution.py:108
  15.3 5.5 %select_add_fusion.1 = f32[32,32,128]{2,1,0:T(8,128)S(1)} fusion(pred[32,32,128]{2,1,0:T(8,128)(4,1)S(1)} %get-tuple-element.337, pred[32,32,128]{2,1,0:T(8,128)(4,1)S(1)} %get-tuple-element.336, pred[32,32,128]{2,1,0:T(8,128)(4,1)S(1)} %get-tuple-element.335, pred[32,32,128]{2,1,0:T(8,128)(4,1)S(1)} %get-tuple-element.334, ...), kind=kLoop, calls=%fused_computation.190 | loop fusion | flops 1966080 | bytes 1572896 | tf_op jit(solution)/shard_map/add | solution.py:107
  20.7 486.3 %while.17 = (s32[]{:T(128)}, f32[3,32,32,128]{3,2,1,0:T(8,128)S(1)}, f32[3,32,32,128]{3,2,1,0:T(8,128)}, f32[12,32,32,128]{3,2,1,0:T(8,128)}, f32[32,32,128]{2,1...) while((s32[]{:T(128)}, ...), condition=%wide.region_1.2_spmd.clone.clone.clone, body=%wide.region_0.1_spmd.clone.clone.clone.sunk | while | flops 24403200 | bytes 139880272 | solution.py:190
  72.2 3.6 collective-permute-start.2
  129.1 3.6 collective-permute-start.3
  132.8 3.6 collective-permute-start.2
  159.4 3.6 collective-permute-start.3
  163.1 3.6 collective-permute-start.2
  189.7 3.6 collective-permute-start.3
  193.4 3.6 collective-permute-start.2
  220.0 3.6 collective-permute-start.3
  250.3 3.6 collective-permute-start.3
  254.0 3.6 collective-permute-start.2
  280.6 3.6 collective-permute-start.3
  284.3 3.6 collective-permute-start.2
  310.9 3.6 collective-permute-start.3
  314.6 3.6 collective-permute-start.2
  341.2 3.6 collective-permute-start.3
  371.5 3.6 collective-permute-start.3
  401.8 3.6 collective-permute-start.3
  432.1 3.6 collective-permute-start.3
  462.4 3.6 collective-permute-start.3
  492.7 3.6 collective-permute-start.3
  (1277 shorter events, 409.6 us)
Async XLA Ops:
  20.8 10.3 %collective-permute-start.1 = (f32[2,32,1,128]{3,2,1,0:T(1,128)S(1)}, f32[2,32,1,128]{3,2,1,0:T(1,128)S(1)}, u32[]{:S(2)}, u32[]{:S(2)}) collective-permute-start(f32[2,32,1,128]{3,2,1,0:T(1,128)S(1)} %slice.599), channel_id=1, source_target_pairs={{1,0},{2,1},{3,2},{4,3},{5,4},{6,5},{7,6},{9,8},{10,9},{11,10},{12... | collective-permute-start | bytes 98312 | tf_op jit(solution)/shard_map/while/body/eval_jaxpr/ppermute | solution.py:21
  23.4 7.7 %collective-permute-start = (f32[2,1,32,128]{3,2,1,0:T(8,128)S(1)}, f32[2,1,32,128]{3,2,1,0:T(8,128)S(1)}, u32[]{:S(2)}, u32[]{:S(2)}) collective-permute-start(f32[2,1,32,128]{3,2,1,0:T(8,128)S(1)} %slice.596), channel_id=1, source_target_pairs={{8,0},{16,8},{24,16},{9,1},{17,9},{25,17},{10,2},{18,10},{26,18},{... | collective-permute-start | bytes 98312 | tf_op jit(solution)/shard_map/while/body/eval_jaxpr/ppermute | solution.py:21
  52.6 8.6 %collective-permute-start.1 = (f32[2,32,1,128]{3,2,1,0:T(1,128)S(1)}, f32[2,32,1,128]{3,2,1,0:T(1,128)S(1)}, u32[]{:S(2)}, u32[]{:S(2)}) collective-permute-start(f32[2,32,1,128]{3,2,1,0:T(1,128)S(1)} %slice.599), channel_id=1, source_target_pairs={{1,0},{2,1},{3,2},{4,3},{5,4},{6,5},{7,6},{9,8},{10,9},{11,10},{12... | collective-permute-start | bytes 98312 | tf_op jit(solution)/shard_map/while/body/eval_jaxpr/ppermute | solution.py:21
  82.9 8.5 %collective-permute-start.1 = (f32[2,32,1,128]{3,2,1,0:T(1,128)S(1)}, f32[2,32,1,128]{3,2,1,0:T(1,128)S(1)}, u32[]{:S(2)}, u32[]{:S(2)}) collective-permute-start(f32[2,32,1,128]{3,2,1,0:T(1,128)S(1)} %slice.599), channel_id=1, source_target_pairs={{1,0},{2,1},{3,2},{4,3},{5,4},{6,5},{7,6},{9,8},{10,9},{11,10},{12... | collective-permute-start | bytes 98312 | tf_op jit(solution)/shard_map/while/body/eval_jaxpr/ppermute | solution.py:21
  113.2 8.5 %collective-permute-start.1 = (f32[2,32,1,128]{3,2,1,0:T(1,128)S(1)}, f32[2,32,1,128]{3,2,1,0:T(1,128)S(1)}, u32[]{:S(2)}, u32[]{:S(2)}) collective-permute-start(f32[2,32,1,128]{3,2,1,0:T(1,128)S(1)} %slice.599), channel_id=1, source_target_pairs={{1,0},{2,1},{3,2},{4,3},{5,4},{6,5},{7,6},{9,8},{10,9},{11,10},{12... | collective-permute-start | bytes 98312 | tf_op jit(solution)/shard_map/while/body/eval_jaxpr/ppermute | solution.py:21
  129.1 7.4 %collective-permute-start.3 = (f32[2,32,1,128]{3,2,1,0:T(1,128)S(1)}, f32[2,32,1,128]{3,2,1,0:T(1,128)S(1)}, u32[]{:S(2)}, u32[]{:S(2)}) collective-permute-start(f32[2,32,1,128]{3,2,1,0:T(1,128)S(1)} %slice.601), channel_id=1, source_target_pairs={{0,1},{1,2},{2,3},{3,4},{4,5},{5,6},{6,7},{8,9},{9,10},{10,11},{11... | collective-permute-start | bytes 98312 | tf_op jit(solution)/shard_map/while/body/eval_jaxpr/ppermute | solution.py:21
  143.5 8.5 %collective-permute-start.1 = (f32[2,32,1,128]{3,2,1,0:T(1,128)S(1)}, f32[2,32,1,128]{3,2,1,0:T(1,128)S(1)}, u32[]{:S(2)}, u32[]{:S(2)}) collective-permute-start(f32[2,32,1,128]{3,2,1,0:T(1,128)S(1)} %slice.599), channel_id=1, source_target_pairs={{1,0},{2,1},{3,2},{4,3},{5,4},{6,5},{7,6},{9,8},{10,9},{11,10},{12... | collective-permute-start | bytes 98312 | tf_op jit(solution)/shard_map/while/body/eval_jaxpr/ppermute | solution.py:21
  159.4 7.4 %collective-permute-start.3 = (f32[2,32,1,128]{3,2,1,0:T(1,128)S(1)}, f32[2,32,1,128]{3,2,1,0:T(1,128)S(1)}, u32[]{:S(2)}, u32[]{:S(2)}) collective-permute-start(f32[2,32,1,128]{3,2,1,0:T(1,128)S(1)} %slice.601), channel_id=1, source_target_pairs={{0,1},{1,2},{2,3},{3,4},{4,5},{5,6},{6,7},{8,9},{9,10},{10,11},{11... | collective-permute-start | bytes 98312 | tf_op jit(solution)/shard_map/while/body/eval_jaxpr/ppermute | solution.py:21
  173.8 8.5 %collective-permute-start.1 = (f32[2,32,1,128]{3,2,1,0:T(1,128)S(1)}, f32[2,32,1,128]{3,2,1,0:T(1,128)S(1)}, u32[]{:S(2)}, u32[]{:S(2)}) collective-permute-start(f32[2,32,1,128]{3,2,1,0:T(1,128)S(1)} %slice.599), channel_id=1, source_target_pairs={{1,0},{2,1},{3,2},{4,3},{5,4},{6,5},{7,6},{9,8},{10,9},{11,10},{12... | collective-permute-start | bytes 98312 | tf_op jit(solution)/shard_map/while/body/eval_jaxpr/ppermute | solution.py:21
  189.7 7.4 %collective-permute-start.3 = (f32[2,32,1,128]{3,2,1,0:T(1,128)S(1)}, f32[2,32,1,128]{3,2,1,0:T(1,128)S(1)}, u32[]{:S(2)}, u32[]{:S(2)}) collective-permute-start(f32[2,32,1,128]{3,2,1,0:T(1,128)S(1)} %slice.601), channel_id=1, source_target_pairs={{0,1},{1,2},{2,3},{3,4},{4,5},{5,6},{6,7},{8,9},{9,10},{10,11},{11... | collective-permute-start | bytes 98312 | tf_op jit(solution)/shard_map/while/body/eval_jaxpr/ppermute | solution.py:21
  204.1 8.5 %collective-permute-start.1 = (f32[2,32,1,128]{3,2,1,0:T(1,128)S(1)}, f32[2,32,1,128]{3,2,1,0:T(1,128)S(1)}, u32[]{:S(2)}, u32[]{:S(2)}) collective-permute-start(f32[2,32,1,128]{3,2,1,0:T(1,128)S(1)} %slice.599), channel_id=1, source_target_pairs={{1,0},{2,1},{3,2},{4,3},{5,4},{6,5},{7,6},{9,8},{10,9},{11,10},{12... | collective-permute-start | bytes 98312 | tf_op jit(solution)/shard_map/while/body/eval_jaxpr/ppermute | solution.py:21
  220.0 7.4 %collective-permute-start.3 = (f32[2,32,1,128]{3,2,1,0:T(1,128)S(1)}, f32[2,32,1,128]{3,2,1,0:T(1,128)S(1)}, u32[]{:S(2)}, u32[]{:S(2)}) collective-permute-start(f32[2,32,1,128]{3,2,1,0:T(1,128)S(1)} %slice.601), channel_id=1, source_target_pairs={{0,1},{1,2},{2,3},{3,4},{4,5},{5,6},{6,7},{8,9},{9,10},{10,11},{11... | collective-permute-start | bytes 98312 | tf_op jit(solution)/shard_map/while/body/eval_jaxpr/ppermute | solution.py:21
  234.4 8.5 %collective-permute-start.1 = (f32[2,32,1,128]{3,2,1,0:T(1,128)S(1)}, f32[2,32,1,128]{3,2,1,0:T(1,128)S(1)}, u32[]{:S(2)}, u32[]{:S(2)}) collective-permute-start(f32[2,32,1,128]{3,2,1,0:T(1,128)S(1)} %slice.599), channel_id=1, source_target_pairs={{1,0},{2,1},{3,2},{4,3},{5,4},{6,5},{7,6},{9,8},{10,9},{11,10},{12... | collective-permute-start | bytes 98312 | tf_op jit(solution)/shard_map/while/body/eval_jaxpr/ppermute | solution.py:21
  250.3 7.4 %collective-permute-start.3 = (f32[2,32,1,128]{3,2,1,0:T(1,128)S(1)}, f32[2,32,1,128]{3,2,1,0:T(1,128)S(1)}, u32[]{:S(2)}, u32[]{:S(2)}) collective-permute-start(f32[2,32,1,128]{3,2,1,0:T(1,128)S(1)} %slice.601), channel_id=1, source_target_pairs={{0,1},{1,2},{2,3},{3,4},{4,5},{5,6},{6,7},{8,9},{9,10},{10,11},{11... | collective-permute-start | bytes 98312 | tf_op jit(solution)/shard_map/while/body/eval_jaxpr/ppermute | solution.py:21
  264.7 8.5 %collective-permute-start.1 = (f32[2,32,1,128]{3,2,1,0:T(1,128)S(1)}, f32[2,32,1,128]{3,2,1,0:T(1,128)S(1)}, u32[]{:S(2)}, u32[]{:S(2)}) collective-permute-start(f32[2,32,1,128]{3,2,1,0:T(1,128)S(1)} %slice.599), channel_id=1, source_target_pairs={{1,0},{2,1},{3,2},{4,3},{5,4},{6,5},{7,6},{9,8},{10,9},{11,10},{12... | collective-permute-start | bytes 98312 | tf_op jit(solution)/shard_map/while/body/eval_jaxpr/ppermute | solution.py:21
  295.0 8.5 %collective-permute-start.1 = (f32[2,32,1,128]{3,2,1,0:T(1,128)S(1)}, f32[2,32,1,128]{3,2,1,0:T(1,128)S(1)}, u32[]{:S(2)}, u32[]{:S(2)}) collective-permute-start(f32[2,32,1,128]{3,2,1,0:T(1,128)S(1)} %slice.599), channel_id=1, source_target_pairs={{1,0},{2,1},{3,2},{4,3},{5,4},{6,5},{7,6},{9,8},{10,9},{11,10},{12... | collective-permute-start | bytes 98312 | tf_op jit(solution)/shard_map/while/body/eval_jaxpr/ppermute | solution.py:21
  325.3 8.5 %collective-permute-start.1 = (f32[2,32,1,128]{3,2,1,0:T(1,128)S(1)}, f32[2,32,1,128]{3,2,1,0:T(1,128)S(1)}, u32[]{:S(2)}, u32[]{:S(2)}) collective-permute-start(f32[2,32,1,128]{3,2,1,0:T(1,128)S(1)} %slice.599), channel_id=1, source_target_pairs={{1,0},{2,1},{3,2},{4,3},{5,4},{6,5},{7,6},{9,8},{10,9},{11,10},{12... | collective-permute-start | bytes 98312 | tf_op jit(solution)/shard_map/while/body/eval_jaxpr/ppermute | solution.py:21
  341.2 7.4 %collective-permute-start.3 = (f32[2,32,1,128]{3,2,1,0:T(1,128)S(1)}, f32[2,32,1,128]{3,2,1,0:T(1,128)S(1)}, u32[]{:S(2)}, u32[]{:S(2)}) collective-permute-start(f32[2,32,1,128]{3,2,1,0:T(1,128)S(1)} %slice.601), channel_id=1, source_target_pairs={{0,1},{1,2},{2,3},{3,4},{4,5},{5,6},{6,7},{8,9},{9,10},{10,11},{11... | collective-permute-start | bytes 98312 | tf_op jit(solution)/shard_map/while/body/eval_jaxpr/ppermute | solution.py:21
  355.6 8.5 %collective-permute-start.1 = (f32[2,32,1,128]{3,2,1,0:T(1,128)S(1)}, f32[2,32,1,128]{3,2,1,0:T(1,128)S(1)}, u32[]{:S(2)}, u32[]{:S(2)}) collective-permute-start(f32[2,32,1,128]{3,2,1,0:T(1,128)S(1)} %slice.599), channel_id=1, source_target_pairs={{1,0},{2,1},{3,2},{4,3},{5,4},{6,5},{7,6},{9,8},{10,9},{11,10},{12... | collective-permute-start | bytes 98312 | tf_op jit(solution)/shard_map/while/body/eval_jaxpr/ppermute | solution.py:21
  385.9 8.5 %collective-permute-start.1 = (f32[2,32,1,128]{3,2,1,0:T(1,128)S(1)}, f32[2,32,1,128]{3,2,1,0:T(1,128)S(1)}, u32[]{:S(2)}, u32[]{:S(2)}) collective-permute-start(f32[2,32,1,128]{3,2,1,0:T(1,128)S(1)} %slice.599), channel_id=1, source_target_pairs={{1,0},{2,1},{3,2},{4,3},{5,4},{6,5},{7,6},{9,8},{10,9},{11,10},{12... | collective-permute-start | bytes 98312 | tf_op jit(solution)/shard_map/while/body/eval_jaxpr/ppermute | solution.py:21
  416.2 8.5 %collective-permute-start.1 = (f32[2,32,1,128]{3,2,1,0:T(1,128)S(1)}, f32[2,32,1,128]{3,2,1,0:T(1,128)S(1)}, u32[]{:S(2)}, u32[]{:S(2)}) collective-permute-start(f32[2,32,1,128]{3,2,1,0:T(1,128)S(1)} %slice.599), channel_id=1, source_target_pairs={{1,0},{2,1},{3,2},{4,3},{5,4},{6,5},{7,6},{9,8},{10,9},{11,10},{12... | collective-permute-start | bytes 98312 | tf_op jit(solution)/shard_map/while/body/eval_jaxpr/ppermute | solution.py:21
  446.5 8.5 %collective-permute-start.1 = (f32[2,32,1,128]{3,2,1,0:T(1,128)S(1)}, f32[2,32,1,128]{3,2,1,0:T(1,128)S(1)}, u32[]{:S(2)}, u32[]{:S(2)}) collective-permute-start(f32[2,32,1,128]{3,2,1,0:T(1,128)S(1)} %slice.599), channel_id=1, source_target_pairs={{1,0},{2,1},{3,2},{4,3},{5,4},{6,5},{7,6},{9,8},{10,9},{11,10},{12... | collective-permute-start | bytes 98312 | tf_op jit(solution)/shard_map/while/body/eval_jaxpr/ppermute | solution.py:21
  462.4 7.4 %collective-permute-start.3 = (f32[2,32,1,128]{3,2,1,0:T(1,128)S(1)}, f32[2,32,1,128]{3,2,1,0:T(1,128)S(1)}, u32[]{:S(2)}, u32[]{:S(2)}) collective-permute-start(f32[2,32,1,128]{3,2,1,0:T(1,128)S(1)} %slice.601), channel_id=1, source_target_pairs={{0,1},{1,2},{2,3},{3,4},{4,5},{5,6},{6,7},{8,9},{9,10},{10,11},{11... | collective-permute-start | bytes 98312 | tf_op jit(solution)/shard_map/while/body/eval_jaxpr/ppermute | solution.py:21
  476.8 8.5 %collective-permute-start.1 = (f32[2,32,1,128]{3,2,1,0:T(1,128)S(1)}, f32[2,32,1,128]{3,2,1,0:T(1,128)S(1)}, u32[]{:S(2)}, u32[]{:S(2)}) collective-permute-start(f32[2,32,1,128]{3,2,1,0:T(1,128)S(1)} %slice.599), channel_id=1, source_target_pairs={{1,0},{2,1},{3,2},{4,3},{5,4},{6,5},{7,6},{9,8},{10,9},{11,10},{12... | collective-permute-start | bytes 98312 | tf_op jit(solution)/shard_map/while/body/eval_jaxpr/ppermute | solution.py:21
  (222 other events, 915.6 us)
where the time goes:
time: 511 us; the launch traced here: 508 us
  starting transfers between devices  178 us (35%)
  other arithmetic  171 us (33%)
  local copies, waits for them, and re-layouts  130 us (25%)
  waiting for transfers between devices  21.1 us (4%)
  loops' own time  7.51 us (1%)
    ppermute x64, starting transfers between devices, shifted_2(): return lax.ppermute(shard, axis, pairs)  178 us
    while x192, other arithmetic  71.7 us
    sub x48, other arithmetic, advance(): magnetic[component] - time_step * curl_h[component]  49 us
    while x368, local copies, waits for them, and re-layouts  45.1 us
    slice x48, local copies, waits for them, and re-layouts, forward(): shifted = lax.slice_in_dim(field, 1, field.shape[direction], axis=direction)  42.5 us
    another operation x64, other arithmetic, advance(): jnp.stack([keeping * electric[component] + driving * curl_e[component] fo...  29.6 us
    concatenate x16, local copies, waits for them, and re-layouts, forward(): return jnp.concatenate([shifted, following], axis=direction) - field  23.8 us
    ppermute x64, waiting for transfers between devices, shifted_2(): return lax.ppermute(shard, axis, pairs)  21.1 us
  transfers between devices with their start and end apart: 64, of which 16 were waited for; matrix products, arithmetic and copies ran while one was open for 17% of the time, Pallas kernels for 0%

commit v1 on v0

v1 whole, which is shorter than its diff:
```python
import jax
import jax.numpy as jnp
from jax import lax
from jax.experimental import pallas as pl
from jax.experimental.pallas import tpu as pltpu
from jax.sharding import PartitionSpec as P

PML = 16
STEPS = 16
NMAT = 8
SUB = 8
GROUP = 4

time_step = 0.5
sigma_peak = 3.0
kappa_peak = 5.0
alpha_peak = 0.05
MESH = pl.DeviceIdType.MESH


def profile(index, extent, shift_half):
    position = index.astype(jnp.float32) + shift_half
    slab_width = float(PML)
    depth_frac = jnp.maximum(
        jnp.maximum(
            (slab_width - position) / slab_width, (position - (extent - slab_width)) / slab_width
        ),
        0.0,
    )
    depth_cube = depth_frac * depth_frac * depth_frac
    sigma_value = sigma_peak * depth_cube
    kappa_value = 1.0 + (kappa_peak - 1.0) * depth_cube
    alpha_value = alpha_peak * (1.0 - depth_frac)
    decays = jnp.exp(-(sigma_value / kappa_value + alpha_value) * time_step)
    scaling = (
        sigma_value * (decays - 1.0) / (kappa_value * (sigma_value + kappa_value * alpha_value))
    )
    inside_slab = depth_frac > 0.0
    return (
        jnp.where(inside_slab, decays, 0.0),
        jnp.where(inside_slab, scaling, 0.0),
        1.0 / kappa_value,
    )


def make_kernel(size_x, size_y, rows_x, rows_y, depth_z):
    groups = rows_x // GROUP
    tiles = rows_y // SUB
    top, right = rows_x - 1, rows_y - 1

    def kernel(
        e_in, h_in, p_in, m_in, eps_ref, sig_ref, e_out, h_out, p_out,
        E, H, S, keep, drive, mat, cx, cy,
        t_ex, t_ey, t_ax, t_ay, t_c0, t_c1,
        r_ex, r_ey, r_ax, r_ay, r_c0, r_c1,
        in_sem, out_sem, send_sem, recv_sem,
    ):
        gx, gy = lax.axis_index("gx"), lax.axis_index("gy")
        has_lx, has_hx = gx > 0, gx < size_x - 1
        has_ly, has_hy = gy > 0, gy < size_y - 1
        slab_x = (gx == 0, gx == size_x - 1)
        slab_y = (gy == 0, gy == size_y - 1)
        lx, hx, ly, hy = gx - 1, gx + 1, gy - 1, gy + 1
        both = jnp.logical_and
        links = (
            (has_lx, (lx, gy)),
            (has_hx, (hx, gy)),
            (has_ly, (gx, ly)),
            (has_hy, (gx, hy)),
            (both(has_hx, has_ly), (hx, ly)),
            (both(has_lx, has_hy), (lx, hy)),
        )

        plain = [
            (e_in, E.at[:, pl.ds(0, rows_x), pl.ds(0, rows_y), :]),
            (h_in, H.at[:, pl.ds(1, rows_x), pl.ds(SUB, rows_y), :]),
            (m_in, mat),
            (p_in.at[pl.ds(1, 2)], S.at[pl.ds(1, 2)]),
            (p_in.at[pl.ds(7, 2)], S.at[pl.ds(7, 2)]),
        ]
        copies = [pltpu.make_async_copy(a, b, in_sem.at[n]) for n, (a, b) in enumerate(plain)]
        for c in copies:
            c.start()

        def slab_copies(side):
            half_x = pl.ds(side * PML, PML)
            xs = [
                pltpu.make_async_copy(
                    p_in.at[pl.ds(s, 2), half_x], S.at[pl.ds(s, 2), half_x], in_sem.at[5 + n]
                )
                for n, s in enumerate((3, 9))
            ]
            ys = [
                pltpu.make_async_copy(
                    p_in.at[s, :, half_x], S.at[s, :, half_x], in_sem.at[7 + n]
                )
                for n, s in enumerate((0, 5, 6, 11))
            ]
            return xs, ys

        for side in (0, 1):
            xs, ys = slab_copies(side)

            @pl.when(slab_x[side])
            def _():
                for c in xs:
                    c.start()

            @pl.when(slab_y[side])
            def _():
                for c in ys:
                    c.start()

        for ref in (r_ex, r_ey, r_ax, r_ay, r_c0, r_c1):
            ref[...] = jnp.zeros(ref.shape, jnp.float32)

        barrier = pltpu.get_barrier_semaphore()
        for present, target in links:

            @pl.when(present)
            def _():
                pl.semaphore_signal(barrier, inc=1, device_id=target, device_id_type=MESH)

        zero = jnp.zeros((SUB, depth_z), jnp.float32)
        for side in (0, 1):

            @pl.when(jnp.logical_not(slab_x[side]))
            def _():
                @pl.loop(side * PML, side * PML + PML)
                def _(i):
                    for s in (3, 4, 9, 10):
                        S[s, i] = jnp.zeros((rows_y, depth_z), jnp.float32)

            @pl.when(jnp.logical_not(slab_y[side]))
            def _():
                @pl.loop(0, rows_x)
                def _(i):
                    for s in (0, 5, 6, 11):
                        S[s, i, pl.ds(side * PML, PML), :] = jnp.zeros(
                            (PML, depth_z), jnp.float32
                        )

        for c in range(3):
            for t in range(tiles):
                E[c, rows_x, pl.ds(t * SUB, SUB), :] = zero
                H[c, 0, pl.ds(SUB + t * SUB, SUB), :] = zero

        @pl.loop(0, rows_x)
        def _(i):
            for c in range(3):
                E[c, i, pl.ds(rows_y, SUB), :] = zero
                H[c, i + 1, pl.ds(0, SUB), :] = zero

        lane = lax.broadcasted_iota(jnp.int32, (SUB, depth_z), 1)
        row = lax.broadcasted_iota(jnp.int32, (rows_y, depth_z), 0)
        plane = lax.broadcasted_iota(jnp.int32, (rows_x, SUB, depth_z), 0)
        zc = []
        for k, shift in enumerate((0.5, 0.0)):
            zc.append(profile(lane, depth_z, shift))
            for n, v in enumerate(profile(row + gy * rows_y, size_y * rows_y, shift)):
                cy[k, n] = v
            for n, v in enumerate(profile(plane + gx * rows_x, size_x * rows_x, shift)):
                cx[k, n] = v
        not_last = lane < depth_z - 1
        not_first = lane > 0

        keep_vals, drive_vals = [], []
        for m in range(NMAT):
            eps = jnp.full((SUB, depth_z), eps_ref[m], jnp.float32)
            sig = jnp.full((SUB, depth_z), sig_ref[m], jnp.float32)
            loss = sig * time_step / (2.0 * eps)
            keep_vals.append((1.0 - loss) / (1.0 + loss))
            drive_vals.append((time_step / eps) / (1.0 + loss))
        copies[2].wait()

        @pl.loop(0, rows_x)
        def _(i):
            for t in range(tiles):
                rows = pl.ds(t * SUB, SUB)
                number = mat[i, rows, :]
                kv, dv = keep_vals[0], drive_vals[0]
                for m in range(1, NMAT):
                    chosen = number == m
                    kv = jnp.where(chosen, keep_vals[m], kv)
                    dv = jnp.where(chosen, drive_vals[m], dv)
                keep[i, rows, :] = kv
                drive[i, rows, :] = dv

        for n in (0, 1, 3, 4):
            copies[n].wait()
        for side in (0, 1):
            xs, ys = slab_copies(side)

            @pl.when(slab_x[side])
            def _():
                for c in xs:
                    c.wait()

            @pl.when(slab_y[side])
            def _():
                for c in ys:
                    c.wait()

        pl.semaphore_wait(barrier, sum(jnp.where(present, 1, 0) for present, _t in links))

        def term(slot, i, rows, d, coef):
            b, a, q = coef
            renewed = b * S[slot, i, rows, :] + a * d
            S[slot, i, rows, :] = renewed
            return q * d + renewed

        def h_tile(i, y, in_x, in_y):
            rows = pl.ds(y, SUB)
            e0, e1, e2 = (E[c, i, rows, :] for c in range(3))
            dx1 = E[1, i + 1, rows, :] - e1
            dx2 = E[2, i + 1, rows, :] - e2
            nxt = pl.ds(y + 1, SUB)
            dy0 = E[0, i, nxt, :] - e0
            dy2 = E[2, i, nxt, :] - e2
            dz0 = jnp.where(not_last, pltpu.roll(e0, depth_z - 1, 1), 0.0) - e0
            dz1 = jnp.where(not_last, pltpu.roll(e1, depth_z - 1, 1), 0.0) - e1
            t1 = term(1, i, rows, dz1, zc[0])
            t2 = term(2, i, rows, dz0, zc[0])
            if in_x:
                coef = tuple(cx[0, n, i] for n in range(3))
                dx2 = term(3, i, rows, dx2, coef)
                dx1 = term(4, i, rows, dx1, coef)
            if in_y:
                coef = tuple(cy[0, n, rows, :] for n in range(3))
                dy2 = term(0, i, rows, dy2, coef)
                dy0 = term(5, i, rows, dy0, coef)
            out = pl.ds(y + SUB, SUB)
            H[0, i + 1, out, :] = H[0, i + 1, out, :] - time_step * (dy2 - t1)
            H[1, i + 1, out, :] = H[1, i + 1, out, :] - time_step * (t2 - dx2)
            H[2, i + 1, out, :] = H[2, i + 1, out, :] - time_step * (dx1 - dy0)

        def e_tile(i, y, in_x, in_y):
            rows = pl.ds(y, SUB)
            at = pl.ds(y + SUB, SUB)
            prv = pl.ds(y + SUB - 1, SUB)
            h0, h1, h2 = (H[c, i + 1, at, :] for c in range(3))
            dx1 = h1 - H[1, i, at, :]
            dx2 = h2 - H[2, i, at, :]
            dy0 = h0 - H[0, i + 1, prv, :]
            dy2 = h2 - H[2, i + 1, prv, :]
            dz0 = h0 - jnp.where(not_first, pltpu.roll(h0, 1, 1), 0.0)
            dz1 = h1 - jnp.where(not_first, pltpu.roll(h1, 1, 1), 0.0)
            t7 = term(7, i, rows, dz1, zc[1])
            t8 = term(8, i, rows, dz0, zc[1])
            if in_x:
                coef = tuple(cx[1, n, i] for n in range(3))
                dx2 = term(9, i, rows, dx2, coef)
                dx1 = term(10, i, rows, dx1, coef)
            if in_y:
                coef = tuple(cy[1, n, rows, :] for n in range(3))
                dy2 = term(6, i, rows, dy2, coef)
                dy0 = term(11, i, rows, dy0, coef)
            k, d = keep[i, rows, :], drive[i, rows, :]
            E[0, i, rows, :] = k * E[0, i, rows, :] + d * (dy2 - t7)
            E[1, i, rows, :] = k * E[1, i, rows, :] + d * (t8 - dx2)
            E[2, i, rows, :] = k * E[2, i, rows, :] + d * (dx1 - dy0)

        def unit(tile_fn, g, t):
            low_x, low_y = g * GROUP < PML, t * SUB < PML
            px = jnp.where(low_x, slab_x[0], slab_x[1])
            py = jnp.where(low_y, slab_y[0], slab_y[1])
            y = pl.multiple_of(t * SUB, SUB)
            for in_x in (False, True):
                for in_y in (False, True):

                    @pl.when(both(px == in_x, py == in_y))
                    def _():
                        for u in range(GROUP):
                            tile_fn(g * GROUP + u, y, in_x, in_y)

        def exchange(s):
            moves = (
                (has_lx, (lx, gy), has_hx, t_ex, r_ex),
                (has_ly, (gx, ly), has_hy, t_ey, r_ey),
                (both(has_hx, has_ly), (hx, ly), both(has_lx, has_hy), t_c0, r_c0),
                (both(has_lx, has_hy), (lx, hy), both(has_hx, has_ly), t_c1, r_c1),
                (has_hx, (hx, gy), has_lx, t_ax, r_ax),
                (has_hy, (gx, hy), has_ly, t_ay, r_ay),
            )
            return [
                (
                    sends,
                    gets,
                    pltpu.make_async_remote_copy(
                        src_ref=src,
                        dst_ref=dst.at[s],
                        send_sem=send_sem.at[n],
                        recv_sem=recv_sem.at[n, s],
                        device_id=target,
                        device_id_type=MESH,
                    ),
                )
                for n, (sends, target, gets, src, dst) in enumerate(moves)
            ]

        own = pl.ds(0, rows_y)
        inner = pl.ds(SUB, rows_y)

        def advance(step, carry):
            s = lax.rem(step, 2)
            moves = exchange(s)
            t_ex[0] = E[1, 0, own, :]
            t_ex[1] = E[2, 0, own, :]
            t_c0[...] = E[0, top, pl.ds(0, SUB), :]
            t_c1[...] = E[1, 0, pl.ds(rows_y - SUB, SUB), :]
            for i in range(rows_x):
                t_ey[0, pl.ds(i, 1), :] = E[0, i, pl.ds(0, 1), :]
                t_ey[1, pl.ds(i, 1), :] = E[2, i, pl.ds(0, 1), :]
            for sends, _g, copy in moves[:4]:

                @pl.when(sends)
                def _():
                    copy.start()

            @pl.loop(0, tiles + groups - 1)
            def _(k):
                face = k < tiles
                unit(
                    h_tile, jnp.where(face, groups - 1, k - tiles), jnp.where(face, k, tiles - 1)
                )

            t_ax[0] = H[1, rows_x, inner, :]
            t_ax[1] = H[2, rows_x, inner, :]
            for i in range(rows_x):
                t_ay[0, pl.ds(i, 1), :] = H[0, i + 1, pl.ds(SUB + right, 1), :]
                t_ay[1, pl.ds(i, 1), :] = H[2, i + 1, pl.ds(SUB + right, 1), :]
            for sends, _g, copy in moves[4:]:

                @pl.when(sends)
                def _():
                    copy.start()

            @pl.loop(0, (groups - 1) * (tiles - 1))
            def _(k):
                unit(h_tile, lax.div(k, tiles - 1), lax.rem(k, tiles - 1))

            @pl.loop(0, (groups - 2) * (tiles - 2))
            def _(k):
                unit(e_tile, 1 + lax.div(k, tiles - 2), 1 + lax.rem(k, tiles - 2))

            for _s, gets, copy in moves:

                @pl.when(gets)
                def _():
                    copy.wait_recv()

            half = time_step

            @pl.when(has_hx)
            def _():
                H[1, rows_x, inner, :] = H[1, rows_x, inner, :] + half * r_ex[s, 1]
                H[2, rows_x, inner, :] = H[2, rows_x, inner, :] - half * r_ex[s, 0]

            @pl.when(has_hy)
            def _():
                edge = pl.ds(SUB + right, 1)
                for i in range(rows_x):
                    H[0, i + 1, edge, :] = (
                        H[0, i + 1, edge, :] - half * r_ey[s, 1, pl.ds(i, 1), :]
                    )
                    H[2, i + 1, edge, :] = (
                        H[2, i + 1, edge, :] + half * r_ey[s, 0, pl.ds(i, 1), :]
                    )

            @pl.when(has_lx)
            def _():
                H[1, 0, inner, :] = r_ax[s, 0] + half * E[2, 0, own, :]
                H[2, 0, inner, :] = r_ax[s, 1] - half * E[1, 0, own, :]
                edge = pl.ds(SUB + right, 1)
                H[2, 0, edge, :] = H[2, 0, edge, :] + half * r_c0[s, pl.ds(0, 1), :]

            @pl.when(has_ly)
            def _():
                edge = pl.ds(SUB - 1, 1)
                first = pl.ds(0, 1)
                for i in range(rows_x):
                    line = pl.ds(i, 1)
                    H[0, i + 1, edge, :] = r_ay[s, 0, line, :] - half * E[2, i, first, :]
                    H[2, i + 1, edge, :] = r_ay[s, 1, line, :] + half * E[0, i, first, :]
                H[2, rows_x, edge, :] = (
                    H[2, rows_x, edge, :] - half * r_c1[s, pl.ds(SUB - 1, 1), :]
                )

            @pl.loop(0, 2 * groups + 2 * (tiles - 2))
            def _(k):
                side = k < 2 * groups
                j = k - 2 * groups
                g = jnp.where(side, lax.rem(k, groups), (groups - 1) * lax.rem(j, 2))
                t = jnp.where(side, (tiles - 1) * lax.div(k, groups), 1 + lax.div(j, 2))
                unit(e_tile, g, t)

            for sends, _g, copy in moves:

                @pl.when(sends)
                def _():
                    copy.wait_send()

            return carry

        lax.fori_loop(0, STEPS, advance, 0)

        outs = [
            pltpu.make_async_copy(
                E.at[:, pl.ds(0, rows_x), pl.ds(0, rows_y), :], e_out, out_sem.at[0]
            ),
            pltpu.make_async_copy(
                H.at[:, pl.ds(1, rows_x), pl.ds(SUB, rows_y), :], h_out, out_sem.at[1]
            ),
            pltpu.make_async_copy(S, p_out, out_sem.at[2]),
        ]
        for c in outs:
            c.start()
        for c in outs:
            c.wait()

    return kernel


def solution(mesh):
    size_x, size_y = mesh.shape["gx"], mesh.shape["gy"]

    def shards(e_field, h_field, psi, material, eps_table, sigma_table):
        _, rows_x, rows_y, depth_z = e_field.shape
        assert rows_x == 2 * PML and rows_y == 2 * PML and size_x > 1 and size_y > 1
        f32 = jnp.float32
        any_space = pl.BlockSpec(memory_space=pl.ANY)
        smem = pl.BlockSpec(memory_space=pltpu.SMEM)
        face_x = (2, rows_y, depth_z)
        face_y = (2, rows_x, depth_z)
        corner = (SUB, depth_z)
        faces = (face_x, face_y, face_x, face_y, corner, corner)
        padded = (3, rows_x + 1, rows_y + SUB, depth_z)
        cell = (rows_x, rows_y, depth_z)
        return pl.pallas_call(
            make_kernel(size_x, size_y, rows_x, rows_y, depth_z),
            out_shape=[jax.ShapeDtypeStruct(a.shape, f32) for a in (e_field, h_field, psi)],
            in_specs=[any_space] * 4 + [smem] * 2,
            out_specs=[any_space] * 3,
            scratch_shapes=[
                pltpu.VMEM(padded, f32),
                pltpu.VMEM(padded, f32),
                pltpu.VMEM(psi.shape, f32),
                pltpu.VMEM(cell, f32),
                pltpu.VMEM(cell, f32),
                pltpu.VMEM(cell, jnp.int32),
                pltpu.VMEM((2, 3, rows_x, SUB, depth_z), f32),
                pltpu.VMEM((2, 3, rows_y, depth_z), f32),
            ]
            + [pltpu.VMEM(f, f32) for f in faces]
            + [pltpu.VMEM((2,) + f, f32) for f in faces]
            + [
                pltpu.SemaphoreType.DMA((11,)),
                pltpu.SemaphoreType.DMA((3,)),
                pltpu.SemaphoreType.DMA((6,)),
                pltpu.SemaphoreType.DMA((6, 2)),
            ],
            compiler_params=pltpu.CompilerParams(collective_id=0, has_side_effects=True),
        )(e_field, h_field, psi, material, eps_table, sigma_table)

    split = P(None, "gx", "gy", None)
    return jax.shard_map(
        shards,
        mesh=mesh,
        in_specs=(split, split, split, P("gx", "gy", None), P(), P()),
        out_specs=(split, split, split),
        check_vma=False,
    )
```

time: 511 us -> 141 us (0.28)
  starting transfers between devices: 178 us -> 0 us
  other arithmetic: 171 us -> 0 us
  Pallas kernels: 0 us -> 129 us
  local copies, waits for them, and re-layouts: 130 us -> 10.1 us
  waiting for transfers between devices: 21.1 us -> 0 us
  loops' own time: 7.51 us -> 0 us
    ppermute x64 -> x0, starting transfers between devices: 178 us -> none  [shifted_2(): return lax.ppermute(shard, axis, pairs)]
    pallas_call x0 -> x1, Pallas kernels: none -> 129 us  [shards(): pl.pallas_call(make_kernel(size_x, size_y, rows_x, rows_y, depth_z), out_...]
    while x192 -> x0, other arithmetic: 71.7 us -> none
    sub x48 -> x0, other arithmetic: 49 us -> none  [advance(): magnetic[component] - time_step * curl_h[component]]
    slice x178 -> x0, local copies, waits for them, and re-layouts: 46.7 us -> none  [the longest x48 42.5 us: forward(): shifted = lax.slice_in_dim(field, 1, field.shape[direction], axis=direction)]
    while x368 -> x0, local copies, waits for them, and re-layouts: 45.1 us -> none
    another operation x112 -> x0, other arithmetic: 35 us -> none  [the longest x64 29.6 us: advance(): jnp.stack([keeping * electric[component] + driving * curl_e[component] fo...]
    concatenate x48 -> x0, local copies, waits for them, and re-layouts: 27.5 us -> none  [the longest x16 23.8 us: forward(): return jnp.concatenate([shifted, following], axis=direction) - field]
  transfers between devices with their start and end apart: 64 -> 0, of which waited for: 16 -> 0; matrix products, arithmetic and copies ran while one was open for 17% -> 0% of each run, Pallas kernels for 0% -> 0%
where the time goes in v1:
time: 141 us; the launch traced here: 140 us
  Pallas kernels  129 us (91%)
  local copies, waits for them, and re-layouts  10.1 us (7%)
    pallas_call x1, Pallas kernels, shards(): pl.pallas_call(make_kernel(size_x, size_y, rows_x, rows_y, depth_z), out_...  129 us
    unnamed x5, local copies, waits for them, and re-layouts  10.1 us

profile of v1, /device:TPU:5, one launch (start us, length us, event | category | flops | bytes accessed | tf_op | source)
XLA Modules:
  0.0 140.0 jit_solution(9941515663755977417)
XLA Ops:
  0.6 129.2 %shard_map.85 = (f32[3,32,32,128]{3,2,1,0:T(8,128)}, f32[3,32,32,128]{3,2,1,0:T(8,128)}, f32[12,32,32,128]{3,2,1,0:T(8,128)}) custom-call(f32[3,32,32,128]{3,2,1,0:T(8,128)} %e_in.1, f32[3,32,32,128]{3,2,1,0:T(8,128)} %h_in.1, f32[12,32,32,128]{3,2,1,0:T(8,128)} %p_in.1, s32[32,32,128]{2,1,0:T(8,128)} %m_in.1, f32[8]{0:T(128)} %eps_ref.1, f32[8]{0:T(128)} %sig_ref.1), custom_call_target="tpu_custom_call" | custom-call | tf_op jit(solution)/shard_map/pallas_call | solution.py:439
  129.8 0.0 copy-start
  129.8 2.8 %copy.12 = f32[3,32,32,128]{3,2,1,0:T(8,128)} copy(f32[3,32,32,128]{3,2,1,0:T(8,128)} %get-tuple-element.6) | data formatting | bytes 3145728
  132.6 0.0 copy-done
  132.6 1.1 copy.13
  133.8 6.2 %copy.14 = f32[12,32,32,128]{3,2,1,0:T(8,128)} copy(f32[12,32,32,128]{3,2,1,0:T(8,128)} %get-tuple-element.8) | data formatting | bytes 12582912
Async XLA Ops:
  129.8 2.8 %copy-start = (f32[3,32,32,128]{3,2,1,0:T(8,128)S(1)}, f32[3,32,32,128]{3,2,1,0:T(8,128)}, u32[]{:S(2)}) copy-start(f32[3,32,32,128]{3,2,1,0:T(8,128)} %get-tuple-element.7) | copy-start | bytes 4718596

commit v2 on v1

--- a/solution.py
+++ b/solution.py
@@ -9,7 +9,8 @@
 STEPS = 16
 NMAT = 8
 SUB = 8
-GROUP = 4
+GROUP = 16
+AHEAD = 2
 
 time_step = 0.5
 sigma_peak = 3.0
@@ -49,11 +50,11 @@
     top, right = rows_x - 1, rows_y - 1
 
     def kernel(
-        e_in, h_in, p_in, m_in, eps_ref, sig_ref, e_out, h_out, p_out,
-        E, H, S, keep, drive, mat, cx, cy,
+        e_in, h_in, p_in, m_in, eps_ref, sig_ref, E, H, S,
+        keep, drive, mat, cx, cy,
         t_ex, t_ey, t_ax, t_ay, t_c0, t_c1,
         r_ex, r_ey, r_ax, r_ay, r_c0, r_c1,
-        in_sem, out_sem, send_sem, recv_sem,
+        in_sem, send_sem, recv_sem,
     ):
         gx, gy = lax.axis_index("gx"), lax.axis_index("gy")
         has_lx, has_hx = gx > 0, gx < size_x - 1
@@ -203,75 +204,87 @@
 
         pl.semaphore_wait(barrier, sum(jnp.where(present, 1, 0) for present, _t in links))
 
-        def term(slot, i, rows, d, coef):
+        def term(old, d, coef):
             b, a, q = coef
-            renewed = b * S[slot, i, rows, :] + a * d
-            S[slot, i, rows, :] = renewed
-            return q * d + renewed
-
-        def h_tile(i, y, in_x, in_y):
-            rows = pl.ds(y, SUB)
-            e0, e1, e2 = (E[c, i, rows, :] for c in range(3))
-            dx1 = E[1, i + 1, rows, :] - e1
-            dx2 = E[2, i + 1, rows, :] - e2
-            nxt = pl.ds(y + 1, SUB)
-            dy0 = E[0, i, nxt, :] - e0
-            dy2 = E[2, i, nxt, :] - e2
-            dz0 = jnp.where(not_last, pltpu.roll(e0, depth_z - 1, 1), 0.0) - e0
-            dz1 = jnp.where(not_last, pltpu.roll(e1, depth_z - 1, 1), 0.0) - e1
-            t1 = term(1, i, rows, dz1, zc[0])
-            t2 = term(2, i, rows, dz0, zc[0])
-            if in_x:
-                coef = tuple(cx[0, n, i] for n in range(3))
-                dx2 = term(3, i, rows, dx2, coef)
-                dx1 = term(4, i, rows, dx1, coef)
-            if in_y:
-                coef = tuple(cy[0, n, rows, :] for n in range(3))
-                dy2 = term(0, i, rows, dy2, coef)
-                dy0 = term(5, i, rows, dy0, coef)
-            out = pl.ds(y + SUB, SUB)
-            H[0, i + 1, out, :] = H[0, i + 1, out, :] - time_step * (dy2 - t1)
-            H[1, i + 1, out, :] = H[1, i + 1, out, :] - time_step * (t2 - dx2)
-            H[2, i + 1, out, :] = H[2, i + 1, out, :] - time_step * (dx1 - dy0)
-
-        def e_tile(i, y, in_x, in_y):
-            rows = pl.ds(y, SUB)
-            at = pl.ds(y + SUB, SUB)
-            prv = pl.ds(y + SUB - 1, SUB)
-            h0, h1, h2 = (H[c, i + 1, at, :] for c in range(3))
-            dx1 = h1 - H[1, i, at, :]
-            dx2 = h2 - H[2, i, at, :]
-            dy0 = h0 - H[0, i + 1, prv, :]
-            dy2 = h2 - H[2, i + 1, prv, :]
-            dz0 = h0 - jnp.where(not_first, pltpu.roll(h0, 1, 1), 0.0)
-            dz1 = h1 - jnp.where(not_first, pltpu.roll(h1, 1, 1), 0.0)
-            t7 = term(7, i, rows, dz1, zc[1])
-            t8 = term(8, i, rows, dz0, zc[1])
-            if in_x:
-                coef = tuple(cx[1, n, i] for n in range(3))
-                dx2 = term(9, i, rows, dx2, coef)
-                dx1 = term(10, i, rows, dx1, coef)
-            if in_y:
-                coef = tuple(cy[1, n, rows, :] for n in range(3))
-                dy2 = term(6, i, rows, dy2, coef)
-                dy0 = term(11, i, rows, dy0, coef)
-            k, d = keep[i, rows, :], drive[i, rows, :]
-            E[0, i, rows, :] = k * E[0, i, rows, :] + d * (dy2 - t7)
-            E[1, i, rows, :] = k * E[1, i, rows, :] + d * (t8 - dx2)
-            E[2, i, rows, :] = k * E[2, i, rows, :] + d * (dx1 - dy0)
-
-        def unit(tile_fn, g, t):
+            renewed = b * old + a * d
+            return q * d + renewed, renewed
+
+        def loads(k, i, y, in_x, in_y):
+            rows, at = pl.ds(y, SUB), pl.ds(y + SUB, SUB)
+            first = 6 * k
+            if k == 0:
+                src, j, now, step, line = E, i, rows, 1, pl.ds(y + 1, SUB)
+                old = [H[c, i + 1, at, :] for c in range(3)]
+                mats = ()
+            else:
+                src, j, now, step, line = H, i + 1, at, -1, pl.ds(y + SUB - 1, SUB)
+                old = [E[c, i, rows, :] for c in range(3)]
+                mats = (keep[i, rows, :], drive[i, rows, :])
+            own = [src[c, j, now, :] for c in range(3)]
+            side_x = [src[c, j + step, now, :] for c in (1, 2)]
+            side_y = [src[c, j, line, :] for c in (0, 2)]
+            slots = [1, 2] + ([3, 4] if in_x else []) + ([0, 5] if in_y else [])
+            aux = {n: S[first + n, i, rows, :] for n in slots}
+            coef_x = [cx[k, n, i] for n in range(3)] if in_x else None
+            return own, side_x, side_y, old, mats, aux, coef_x
+
+        def compute(k, values, coef_y):
+            own, (x1, x2), (y0, y2), old, mats, aux, coef_x = values
+            f0, f1, f2 = own
+            if k == 0:
+                dx1, dx2, dy0, dy2 = x1 - f1, x2 - f2, y0 - f0, y2 - f2
+                dz0 = jnp.where(not_last, pltpu.roll(f0, depth_z - 1, 1), 0.0) - f0
+                dz1 = jnp.where(not_last, pltpu.roll(f1, depth_z - 1, 1), 0.0) - f1
+            else:
+                dx1, dx2, dy0, dy2 = f1 - x1, f2 - x2, f0 - y0, f2 - y2
+                dz0 = f0 - jnp.where(not_first, pltpu.roll(f0, 1, 1), 0.0)
+                dz1 = f1 - jnp.where(not_first, pltpu.roll(f1, 1, 1), 0.0)
+            fresh = {}
+            dz1, fresh[1] = term(aux[1], dz1, zc[k])
+            dz0, fresh[2] = term(aux[2], dz0, zc[k])
+            if coef_x is not None:
+                dx2, fresh[3] = term(aux[3], dx2, coef_x)
+                dx1, fresh[4] = term(aux[4], dx1, coef_x)
+            if coef_y is not None:
+                dy2, fresh[0] = term(aux[0], dy2, coef_y)
+                dy0, fresh[5] = term(aux[5], dy0, coef_y)
+            curls = (dy2 - dz1, dz0 - dx2, dx1 - dy0)
+            if k == 0:
+                return [o - time_step * c for o, c in zip(old, curls)], fresh
+            return [mats[0] * o + mats[1] * c for o, c in zip(old, curls)], fresh
+
+        def stores(k, i, y, result):
+            fields, fresh = result
+            for c in range(3):
+                if k == 0:
+                    H[c, i + 1, pl.ds(y + SUB, SUB), :] = fields[c]
+                else:
+                    E[c, i, pl.ds(y, SUB), :] = fields[c]
+            for n, v in fresh.items():
+                S[6 * k + n, i, pl.ds(y, SUB), :] = v
+
+        def run(k, i0, y, in_x, in_y):
+            coef_y = [cy[k, n, pl.ds(y, SUB), :] for n in range(3)] if in_y else None
+            ready = [loads(k, i0 + u, y, in_x, in_y) for u in range(AHEAD)]
+            for u in range(GROUP):
+                if u + AHEAD < GROUP:
+                    ready.append(loads(k, i0 + u + AHEAD, y, in_x, in_y))
+                stores(k, i0 + u, y, compute(k, ready[u], coef_y))
+
+        def unit(k, g, t):
             low_x, low_y = g * GROUP < PML, t * SUB < PML
             px = jnp.where(low_x, slab_x[0], slab_x[1])
             py = jnp.where(low_y, slab_y[0], slab_y[1])
-            y = pl.multiple_of(t * SUB, SUB)
-            for in_x in (False, True):
-                for in_y in (False, True):
-
-                    @pl.when(both(px == in_x, py == in_y))
-                    def _():
-                        for u in range(GROUP):
-                            tile_fn(g * GROUP + u, y, in_x, in_y)
+            i0, y = g * GROUP, pl.multiple_of(t * SUB, SUB)
+
+            def split_y(in_x):
+                lax.cond(
+                    py,
+                    lambda: run(k, i0, y, in_x, True),
+                    lambda: run(k, i0, y, in_x, False),
+                )
+
+            lax.cond(px, lambda: split_y(True), lambda: split_y(False))
 
         def exchange(s):
             moves = (
@@ -321,7 +334,7 @@
             def _(k):
                 face = k < tiles
                 unit(
-                    h_tile, jnp.where(face, groups - 1, k - tiles), jnp.where(face, k, tiles - 1)
+                    0, jnp.where(face, groups - 1, k - tiles), jnp.where(face, k, tiles - 1)
                 )
 
             t_ax[0] = H[1, rows_x, inner, :]
@@ -337,11 +350,11 @@
 
             @pl.loop(0, (groups - 1) * (tiles - 1))
             def _(k):
-                unit(h_tile, lax.div(k, tiles - 1), lax.rem(k, tiles - 1))
+                unit(0, lax.div(k, tiles - 1), lax.rem(k, tiles - 1))
 
             @pl.loop(0, (groups - 2) * (tiles - 2))
             def _(k):
-                unit(e_tile, 1 + lax.div(k, tiles - 2), 1 + lax.rem(k, tiles - 2))
+                unit(1, 1 + lax.div(k, tiles - 2), 1 + lax.rem(k, tiles - 2))
 
             for _s, gets, copy in moves:
 
@@ -392,7 +405,7 @@
                 j = k - 2 * groups
                 g = jnp.where(side, lax.rem(k, groups), (groups - 1) * lax.rem(j, 2))
                 t = jnp.where(side, (tiles - 1) * lax.div(k, groups), 1 + lax.div(j, 2))
-                unit(e_tile, g, t)
+                unit(1, g, t)
 
             for sends, _g, copy in moves:
 
@@ -404,6 +417,11 @@
 
         lax.fori_loop(0, STEPS, advance, 0)
 
+    return kernel
+
+
+def make_writer(rows_x, rows_y):
+    def writer(E, H, S, e_out, h_out, p_out, out_sem):
         outs = [
             pltpu.make_async_copy(
                 E.at[:, pl.ds(0, rows_x), pl.ds(0, rows_y), :], e_out, out_sem.at[0]
@@ -418,7 +436,7 @@
         for c in outs:
             c.wait()
 
-    return kernel
+    return writer
 
 
 def solution(mesh):
@@ -428,7 +446,7 @@
         _, rows_x, rows_y, depth_z = e_field.shape
         assert rows_x == 2 * PML and rows_y == 2 * PML and size_x > 1 and size_y > 1
         f32 = jnp.float32
-        any_space = pl.BlockSpec(memory_space=pl.ANY)
+        any_space = pl.BlockSpec(memory_space=pltpu.HBM)
         smem = pl.BlockSpec(memory_space=pltpu.SMEM)
         face_x = (2, rows_y, depth_z)
         face_y = (2, rows_x, depth_z)
@@ -436,15 +454,13 @@
         faces = (face_x, face_y, face_x, face_y, corner, corner)
         padded = (3, rows_x + 1, rows_y + SUB, depth_z)
         cell = (rows_x, rows_y, depth_z)
-        return pl.pallas_call(
+        vmem = pl.BlockSpec(memory_space=pltpu.VMEM)
+        state = pl.pallas_call(
             make_kernel(size_x, size_y, rows_x, rows_y, depth_z),
-            out_shape=[jax.ShapeDtypeStruct(a.shape, f32) for a in (e_field, h_field, psi)],
+            out_shape=[pltpu.VMEM(padded, f32), pltpu.VMEM(padded, f32), pltpu.VMEM(psi.shape, f32)],
             in_specs=[any_space] * 4 + [smem] * 2,
-            out_specs=[any_space] * 3,
+            out_specs=[vmem] * 3,
             scratch_shapes=[
-                pltpu.VMEM(padded, f32),
-                pltpu.VMEM(padded, f32),
-                pltpu.VMEM(psi.shape, f32),
                 pltpu.VMEM(cell, f32),
                 pltpu.VMEM(cell, f32),
                 pltpu.VMEM(cell, jnp.int32),
@@ -455,12 +471,21 @@
             + [pltpu.VMEM((2,) + f, f32) for f in faces]
             + [
                 pltpu.SemaphoreType.DMA((11,)),
-                pltpu.SemaphoreType.DMA((3,)),
                 pltpu.SemaphoreType.DMA((6,)),
                 pltpu.SemaphoreType.DMA((6, 2)),
             ],
-            compiler_params=pltpu.CompilerParams(collective_id=0, has_side_effects=True),
+            compiler_params=pltpu.CompilerParams(
+                collective_id=0, has_side_effects=True, vmem_limit_bytes=53 << 20
+            ),
         )(e_field, h_field, psi, material, eps_table, sigma_table)
+        return pl.pallas_call(
+            make_writer(rows_x, rows_y),
+            out_shape=[jax.ShapeDtypeStruct(a.shape, f32) for a in (e_field, h_field, psi)],
+            in_specs=[vmem] * 3,
+            out_specs=[any_space] * 3,
+            scratch_shapes=[pltpu.SemaphoreType.DMA((3,))],
+            compiler_params=pltpu.CompilerParams(vmem_limit_bytes=24 << 20),
+        )(*state)
 
     split = P(None, "gx", "gy", None)
     return jax.shard_map(

time: 141 us -> 92.3 us (0.65)
  Pallas kernels: 129 us -> 90.1 us
  local copies, waits for them, and re-layouts: 10.1 us -> 0 us
    pallas_call x1, Pallas kernels: 129 us -> 86.3 us  [shards(): pl.pallas_call(make_kernel(size_x, size_y, rows_x, rows_y, depth_z), out_...]
    unnamed x5 -> x0, local copies, waits for them, and re-layouts: 10.1 us -> none
    pallas_call x0 -> x1, Pallas kernels: none -> 3.77 us  [shards(): pl.pallas_call(make_writer(rows_x, rows_y), out_shape=[jax.ShapeDtypeStru...]
where the time goes in v2:
time: 92.3 us; the launch traced here: 90.7 us
  Pallas kernels  90.1 us (98%)
    pallas_call x1, Pallas kernels, shards(): pl.pallas_call(make_kernel(size_x, size_y, rows_x, rows_y, depth_z), out_...  86.3 us
    pallas_call x1, Pallas kernels, shards(): pl.pallas_call(make_writer(rows_x, rows_y), out_shape=[jax.ShapeDtypeStru...  3.77 us

profile of v2, /device:TPU:5, one launch (start us, length us, event | category | flops | bytes accessed | tf_op | source)
XLA Modules:
  0.0 90.7 jit_solution(15863414629102009045)
XLA Ops:
  0.6 86.3 %shard_map.85 = (f32[3,33,40,128]{3,2,1,0:T(8,128)S(1)}, f32[3,33,40,128]{3,2,1,0:T(8,128)S(1)}, f32[12,32,32,128]{3,2,1,0:T(8,128)S(1)}) custom-call(f32[3,32,32,128]{3,2,1,0:T(8,128)} %e_in.1, f32[3,32,32,128]{3,2,1,0:T(8,128)} %h_in.1, f32[12,32,32,128]{3,2,1,0:T(8,128)} %p_in.1, s32[32,32,128]{2,1,0:T(8,128)} %m_in.1, f32[8]{0:T(128)} %eps_ref.1, f32[8]{0:T(128)} %sig_ref.1), custom_call_target="tpu_custom_call" | custom-call | tf_op jit(solution)/shard_map/pallas_call | solution.py:458
  86.9 3.8 %shard_map.86 = (f32[3,32,32,128]{3,2,1,0:T(8,128)}, f32[3,32,32,128]{3,2,1,0:T(8,128)}, f32[12,32,32,128]{3,2,1,0:T(8,128)}) custom-call(f32[3,33,40,128]{3,2,1,0:T(8,128)S(1)} %get-tuple-element.6.E, f32[3,33,40,128]{3,2,1,0:T(8,128)S(1)} %get-tuple-element.7.H, f32[12,32,32,128]{3,2,1,0:T(8,128)S(1)} %get-tuple-element.8.S), custom_call_target="tpu_custom_call" | custom-call | tf_op jit(solution)/shard_map/pallas_call | solution.py:481
